TPU v7x, 512 devices: a 8x2x16 block of a 8x8x16 slice. The times are simulated.
512 devices in a mesh: groups: 2 (over y), dp: 128 (over z, x), tp: 2 (over core).
Axes of the slice: x: 8, y: 2, z: 16, core: 2. Of those that a mesh axis runs over, the one named last changes fastest.
The devices are a block of a 8x8x16 slice.
Arguments:
- pool: bfloat16 [32768, 4608], P(('groups', 'dp')), parts along dimension 0, may hold values from -10 to 10
- page_holder: int32 [14336], P(('groups', 'dp')), parts along dimension 0, may hold values from 0 to 127, as said below
- page_slot: int32 [14336], P(('groups', 'dp')), parts along dimension 0, may hold values from 0 to 127
- suffix_latent_rows: bfloat16 [256, 9216], P(('groups', 'dp')), parts along dimension 0, may hold values from -5 to 5
- prefill_queries: bfloat16 [256, 128, 4608], P(('groups', 'dp'), None, 'tp'), parts along dimension 0, may hold values from -10 to 10
- suffix_len: int32 [32], P('groups'), parts along dimension 0, may hold values from 1 to 128
- decode_queries: bfloat16 [1024, 36864], P(('groups', 'dp'), 'tp'), parts along dimension 0, may hold values from -10 to 10
- decode_len: int32 [1024], P(('groups', 'dp')), parts along dimension 0, may hold values from 1 to 256
Outputs:
- prefill_output: bfloat16 [256, 128, 4096], P(('groups', 'dp'), None, 'tp'), parts along dimension 0
- decode_out: bfloat16 [1024, 32768], P(('groups', 'dp'), 'tp'), parts along dimension 0
There are 2 independent parts, one for each index of `groups`. A program takes and returns all parts, laid end to end along the dimension named above; each array names one. Nothing has to cross between parts.
Inputs may be any that keep to these rules, and one draw needn't show every extreme that they name: `page_holder`: within one device's 56 entries no holder appears more than 1 times, and some holder appears exactly 1 times.
All inputs are finite; a program needn't handle non-finite values.
Results may differ from a plain program's by a relative error of at most 0.004.
Values may be sent and summed in bfloat16 or wider, within the bound.
A program may use at most 64 MiB of HBM per device.

v0:
```python
import jax
import jax.numpy as jnp
from jax import lax
from jax.sharding import Mesh
from jax.sharding import PartitionSpec as P

LATENT_WIDTH = 512
ROTARY_WIDTH = 64
TEAM_RANKS = 8
SUFFIX_TOKENS = 128
DP = ("dp_0", "dp_1")
GROUPS_DP = ("groups", "dp_0", "dp_1")


softmax_scale = 192.0 ** (-0.5)
masked_score = -1e30


def from_partner(value, axis, stride):
    mask = 2**stride
    pairs = [(source, source ^ mask) for source in range(lax.axis_size(axis))]
    return lax.ppermute(value, axis, pairs)


def in_blocks(array, dim, size):
    before, after = (array.shape[:dim], array.shape[dim + 1 :])
    return jnp.moveaxis(array.reshape(*before, size, -1, *after), dim, 0)


def in_order(parts, dim):
    lengths = list(parts.shape[1:])
    lengths[dim] *= parts.shape[0]
    return jnp.moveaxis(parts, 0, dim).reshape(lengths)


def moved_by_axis(parts, axes, sequence):
    lengths = [lax.axis_size(a) for a in axes]
    parts = parts.reshape(*lengths, *parts.shape[1:])
    for k in sequence:
        parts = lax.all_to_all(parts, axes[k], split_axis=k, concat_axis=k, tiled=True)
    return parts.reshape(-1, *parts.shape[len(axes) :])


def one_axis_at_a_time(array, axes, sequence, split_dim, concat_dim):
    parts = in_blocks(array, split_dim, lax.axis_size(axes))
    return in_order(moved_by_axis(parts, axes, sequence), concat_dim)


def decode_attention(pool, decode_queries, decode_len, compressed_width):
    row_count = decode_queries.shape[0]
    queries = decode_queries.reshape(row_count, -1, compressed_width)
    context_output = pool.reshape(row_count, -1, compressed_width)
    key_count = context_output.shape[1]
    scores = (
        jnp.einsum("bhr,bkr->bhk", queries, context_output, preferred_element_type=jnp.float32)
        * softmax_scale
    )
    allowed = jnp.arange(key_count, dtype=jnp.int32)[None, :] < decode_len[:, None]
    scores = jnp.where(allowed[:, None, :], scores, masked_score)
    row_peak = jnp.max(scores, axis=-1, keepdims=True)
    powers = jnp.exp(scores - row_peak)
    denominator = jnp.sum(powers, axis=-1)
    blended_output = jnp.einsum(
        "bhk,bkc->bhc",
        powers.astype(jnp.bfloat16),
        context_output[:, :, :LATENT_WIDTH],
        preferred_element_type=jnp.float32,
    )
    blended_output = blended_output / denominator[..., None]
    return blended_output.reshape(row_count, -1).astype(jnp.bfloat16)


def collect(own_pages, suffix_page, on_arrival, carried):
    pages_buffer = own_pages[None]
    suffix_buffer = suffix_page[None]
    carried = on_arrival(carried, own_pages)
    for step_bit in range(TEAM_RANKS.bit_length() - 1):
        other_pages, other_suffix = from_partner((pages_buffer, suffix_buffer), DP, step_bit)
        for slot_index in range(other_pages.shape[0]):
            carried = on_arrival(carried, other_pages[slot_index])
        pages_buffer = jnp.concatenate([pages_buffer, other_pages], axis=0)
        suffix_buffer = jnp.concatenate([suffix_buffer, other_suffix], axis=0)
    return (pages_buffer, suffix_buffer, carried)


def shards(
    pool,
    page_holder,
    page_slot,
    suffix_latent_rows,
    prefill_queries,
    suffix_len,
    decode_queries,
    decode_len,
):
    compressed_width = LATENT_WIDTH + ROTARY_WIDTH
    devices = lax.axis_size(DP)
    my_index = lax.axis_index(DP)
    pull_count = page_holder.shape[0]
    capacity = (pull_count + devices - 1) // devices
    share_tokens = suffix_latent_rows.shape[1] // compressed_width
    pull_order = jnp.arange(pull_count, dtype=jnp.int32)
    earlier = (page_holder[None, :] == page_holder[:, None]) & (
        pull_order[None, :] < pull_order[:, None]
    )
    page_rank = jnp.sum(earlier.astype(jnp.int32), axis=1)
    holder_ids = jnp.arange(devices, dtype=jnp.int32)
    slot_ids = jnp.arange(capacity, dtype=jnp.int32)
    matches = (page_holder[None, None, :] == holder_ids[:, None, None]) & (
        page_rank[None, None, :] == slot_ids[None, :, None]
    )
    request = jnp.sum(jnp.where(matches, page_slot[None, None, :] + 1, 0), axis=2) - 1
    wanted = one_axis_at_a_time(request, DP, (0, 1), 0, 0)
    page_rows = pool[jnp.maximum(wanted, 0)]
    page_rows = jnp.where((wanted >= 0)[..., None], page_rows, jnp.zeros((), pool.dtype))
    received = lax.all_to_all(page_rows, DP, split_axis=0, concat_axis=0, tiled=True)
    flat_received = received.reshape(devices * capacity, -1)
    pulled = flat_received[page_holder * capacity + page_rank]
    decode_part = decode_attention(pool, decode_queries, decode_len, compressed_width)
    member = my_index % TEAM_RANKS
    length = lax.dynamic_index_in_dim(suffix_len, my_index // TEAM_RANKS, keepdims=False)
    queries = prefill_queries[0].reshape(SUFFIX_TOKENS, -1, compressed_width)
    head_total = queries.shape[1]
    query_pos = jnp.arange(SUFFIX_TOKENS, dtype=jnp.int32)

    def attend(carried, key_matrix, allowed):
        peak_old, denominator_old, blended_old = carried
        scores = (
            jnp.einsum("shr,kr->shk", queries, key_matrix, preferred_element_type=jnp.float32)
            * softmax_scale
        )
        if allowed is not None:
            scores = jnp.where(allowed[:, None, :], scores, masked_score)
        peak_new = jnp.maximum(peak_old, jnp.max(scores, axis=-1))
        powers = jnp.exp(scores - peak_new[..., None])
        factor = jnp.exp(peak_old - peak_new)
        denominator_new = denominator_old * factor + jnp.sum(powers, axis=-1)
        contribution = jnp.einsum(
            "shk,kc->shc",
            powers.astype(jnp.bfloat16),
            key_matrix[:, :LATENT_WIDTH],
            preferred_element_type=jnp.float32,
        )
        blended_new = blended_old * factor[..., None] + contribution
        return (peak_new, denominator_new, blended_new)

    def unchanged(carried, block):
        return carried

    carried = (
        jnp.full((SUFFIX_TOKENS, head_total), masked_score, jnp.float32),
        jnp.zeros((SUFFIX_TOKENS, head_total), jnp.float32),
        jnp.zeros((SUFFIX_TOKENS, head_total, LATENT_WIDTH), jnp.float32),
    )
    gathered_pages, gathered_suffix, carried = collect(
        pulled, suffix_latent_rows, unchanged, carried
    )
    for slot_index in range(TEAM_RANKS):
        carried = attend(carried, gathered_pages[slot_index].reshape(-1, compressed_width), None)
    members = jnp.bitwise_xor(member, jnp.arange(TEAM_RANKS, dtype=jnp.int32))
    key_pos = (
        members[:, None] * share_tokens + jnp.arange(share_tokens, dtype=jnp.int32)[None, :]
    ).reshape(-1)
    suffix_keys = gathered_suffix.reshape(-1, compressed_width)
    allowed = (key_pos[None, :] <= query_pos[:, None]) & (key_pos[None, :] < length)
    peak_final, denominator, blended_output = attend(carried, suffix_keys, allowed)
    blended_output = blended_output / denominator[..., None]
    blended_output = jnp.where((query_pos < length)[:, None, None], blended_output, 0.0)
    prefill_part = blended_output.reshape(1, SUFFIX_TOKENS, -1).astype(jnp.bfloat16)
    return (prefill_part, decode_part)


def solution(mesh):
    torus = Mesh(
        mesh.devices.reshape(mesh.shape["groups"], 16, 8, mesh.shape["tp"]),
        ("groups", "dp_0", "dp_1", "tp"),
    )
    placed = (
        P(GROUPS_DP, None),
        P(GROUPS_DP),
        P(GROUPS_DP),
        P(GROUPS_DP, None),
        P(GROUPS_DP, None, "tp"),
        P("groups"),
        P(GROUPS_DP, "tp"),
        P(GROUPS_DP),
    )
    return jax.shard_map(
        shards,
        mesh=torus,
        in_specs=placed,
        out_specs=(P(GROUPS_DP, None, "tp"), P(GROUPS_DP, "tp")),
        check_vma=False,
    )
```

profile of v0, /device:TPU:65, one launch (start us, length us, event | category | flops | bytes accessed | tf_op | source)
XLA Modules:
  0.0 348.5 jit_solution(7270344062162224252)
XLA Ops:
  3.1 55.2 %all_to_all.15 = s32[16,8,1,1]{1,3,2,0:T(1,128)S(1)} all-to-all(s32[16,8,1,1]{1,3,2,0:T(1,128)S(1)} %bitcast.118), channel_id=1, replica_groups=mesh['groups'=2,'dp_0'=16,'dp_1'=8,'tp'=2] {'dp_0'}, dimensions={0} | all-to-all | bytes 1024 | tf_op jit(solution)/shard_map/all_to_all | solution.py:40
  58.3 13.4 %all_to_all.16 = s32[16,8,1,1]{0,3,2,1:T(1,128)S(1)} all-to-all(s32[16,8,1,1]{0,3,2,1:T(1,128)S(1)} %copy.62), channel_id=1, replica_groups=mesh['groups'=2,'dp_0'=16,'dp_1'=8,'tp'=2] {'dp_1'}, dimensions={1} | all-to-all | bytes 1024 | tf_op jit(solution)/shard_map/all_to_all | solution.py:40
  72.0 3.8 %gather_fusion = bf16[128,4608]{1,0:T(8,128)(2,1)S(1)} fusion(bf16[128,4608]{1,0:T(8,128)(2,1)} %param.8, s32[1024]{0:T(1024)S(1)} %pad_clamp_fusion.1), kind=kCustom, calls=%fused_computation | custom fusion | bytes 2359808 | tf_op jit(solution)/shard_map/gather | solution.py:114
  76.6 1.5 reduce.1
  79.2 10.7 %all-to-all-start.2 = ((bf16[128,2,2304]{2,1,0:T(2,128)(2,1)}), bf16[128,2,2304]{2,1,0:T(2,128)(2,1)}, u32[]{:S(2)}, u32[]{:S(2)}) async-start(bf16[128,2,2304]{2,1,0:T(2,128)(2,1)} %reshape.581), calls=%async_computation.2 | async-start | bytes 2359296 | tf_op jit(solution)/shard_map/all_to_all | solution.py:116
  90.0 2.1 collective-permute-start.3
  96.2 2.6 collective-permute-start.4
  99.9 40.7 %all-to-all-done.2 = bf16[128,2,2304]{2,1,0:T(2,128)(2,1)} async-done(((bf16[128,2,2304]{2,1,0:T(2,128)(2,1)}), bf16[128,2,2304]{2,1,0:T(2,128)(2,1)}, u32[]{:S(2)}, u32[]{:S(2)}) %all-to-all-start.2) | async-done | bytes 1179680 | tf_op jit(solution)/shard_map/all_to_all | solution.py:116
  140.7 8.0 %reshape.582 = bf16[128,1,4608]{2,1,0:T(2,128)(2,1)} reshape(bf16[128,2,2304]{2,1,0:T(2,128)(2,1)} %all-to-all-done.2) | data formatting | bytes 2359296
  148.7 1.8 copy.81
  151.4 3.2 collective-permute-start
  154.7 7.5 %collective-permute-start.5 = (bf16[4,1,9216]{2,0,1:T(4,128)(2,1)S(1)}, bf16[4,1,9216]{2,0,1:T(4,128)(2,1)S(1)}, u32[]{:S(2)}, u32[]{:S(2)}) collective-permute-start(bf16[4,1,9216]{2,0,1:T(4,128)(2,1)S(1)} %pad_maximum_fusion.3), channel_id=1, source_target_pairs={{0,8},{2,10},{4,12},{6,14},{8,0},{10,2},{12,4},{14,6},{16,24},{18,... | collective-permute-start | bytes 221192 | tf_op jit(solution)/shard_map/ppermute | solution.py:22
  163.4 3.9 %collective-permute-start.1 = (bf16[2,56,4608]{2,1,0:T(8,128)(2,1)}, bf16[2,56,4608]{2,1,0:T(8,128)(2,1)}, u32[]{:S(2)}, u32[]{:S(2)}) collective-permute-start(bf16[2,56,4608]{2,1,0:T(8,128)(2,1)} %pad_maximum_fusion.1), channel_id=1, source_target_pairs={{0,4},{2,6},{4,0},{6,2},{8,12},{10,14},{12,8},{14,10},{16,20},{18,... | collective-permute-start | bytes 3096584 | tf_op jit(solution)/shard_map/ppermute | solution.py:22
  170.2 43.8 %collective-permute-done.1 = bf16[2,56,4608]{2,1,0:T(8,128)(2,1)} collective-permute-done((bf16[2,56,4608]{2,1,0:T(8,128)(2,1)}, bf16[2,56,4608]{2,1,0:T(8,128)(2,1)}, u32[]{:S(2)}, u32[]{:S(2)}) %collective-permute-start.1) | collective-permute-done | bytes 1032224 | tf_op jit(solution)/shard_map/ppermute | solution.py:22
  213.9 2.7 pad_maximum_fusion
  216.6 9.7 %collective-permute-start.2 = (bf16[4,56,4608]{2,1,0:T(8,128)(2,1)}, bf16[4,56,4608]{2,1,0:T(8,128)(2,1)}, u32[]{:S(2)}, u32[]{:S(2)}) collective-permute-start(bf16[4,56,4608]{2,1,0:T(8,128)(2,1)} %pad_maximum_fusion), channel_id=1, source_target_pairs={{0,8},{2,10},{4,12},{6,14},{8,0},{10,2},{12,4},{14,6},{16,24},{18,... | collective-permute-start | bytes 6193160 | tf_op jit(solution)/shard_map/ppermute | solution.py:22
  235.9 1.4 fusion.79
  237.4 1.5 fusion.80
  238.9 77.2 %collective-permute-done.2 = bf16[4,56,4608]{2,1,0:T(8,128)(2,1)} collective-permute-done((bf16[4,56,4608]{2,1,0:T(8,128)(2,1)}, bf16[4,56,4608]{2,1,0:T(8,128)(2,1)}, u32[]{:S(2)}, u32[]{:S(2)}) %collective-permute-start.2) | collective-permute-done | bytes 2064416 | tf_op jit(solution)/shard_map/ppermute | solution.py:22
  316.1 2.6 fusion.72
  318.7 2.3 reshape.563
  321.0 2.3 reshape_squeeze.28
  323.3 2.3 reshape.565
  325.7 2.3 reshape_squeeze.29
  (133 shorter events, 44.7 us)
Async XLA Ops:
  79.2 10.8 %copy-start.19 = (bf16[1,9216]{1,0:T(2,128)(2,1)S(1)}, bf16[1,9216]{1,0:T(2,128)(2,1)}, u32[]{:S(2)}) copy-start(bf16[1,9216]{1,0:T(2,128)(2,1)} %param.11) | copy-start | bytes 55300
  79.2 12.9 %copy-start = (bf16[128,4608]{1,0:T(8,128)(2,1)S(1)}, bf16[128,4608]{1,0:T(8,128)(2,1)}, u32[]{:S(2)}) copy-start(bf16[128,4608]{1,0:T(8,128)(2,1)} %param.8) | copy-start | bytes 3538948
  79.2 61.4 %all-to-all-start.2 = ((bf16[128,2,2304]{2,1,0:T(2,128)(2,1)}), bf16[128,2,2304]{2,1,0:T(2,128)(2,1)}, u32[]{:S(2)}, u32[]{:S(2)}) async-start(bf16[128,2,2304]{2,1,0:T(2,128)(2,1)} %reshape.581), calls=%async_computation.2 | async-start | bytes 2359296 | tf_op jit(solution)/shard_map/all_to_all | solution.py:116
  90.0 3.4 copy-start.20
  90.0 6.1 %collective-permute-start.3 = (bf16[1,1,9216]{2,0,1:T(2,128)(2,1)S(1)}, bf16[1,1,9216]{2,0,1:T(2,128)(2,1)S(1)}, u32[]{:S(2)}, u32[]{:S(2)}) collective-permute-start(bf16[1,1,9216]{2,0,1:T(2,128)(2,1)S(1)} %bitcast.111), channel_id=1, source_target_pairs={{0,2},{2,0},{4,6},{6,4},{8,10},{10,8},{12,14},{14,12},{16,18},{18,... | collective-permute-start | bytes 55304 | tf_op jit(solution)/shard_map/ppermute | solution.py:22
  92.1 1.5 copy-start.22
  92.1 2.1 copy-start.23
  93.2 1.8 copy-start.21
  94.8 4.0 %copy-start.18 = (bf16[1,128,2304]{2,1,0:T(8,128)(2,1)S(1)}, bf16[1,128,2304]{2,1,0:T(8,128)(2,1)}, u32[]{:S(2)}) copy-start(bf16[1,128,2304]{2,1,0:T(8,128)(2,1)} %param.12) | copy-start | bytes 1769476
  96.2 58.4 %collective-permute-start.4 = (bf16[2,1,9216]{2,0,1:T(2,128)(2,1)S(1)}, bf16[2,1,9216]{2,0,1:T(2,128)(2,1)S(1)}, u32[]{:S(2)}, u32[]{:S(2)}) collective-permute-start(bf16[2,1,9216]{2,0,1:T(2,128)(2,1)S(1)} %pad_maximum_fusion.4), channel_id=1, source_target_pairs={{0,4},{2,6},{4,0},{6,2},{8,12},{10,14},{12,8},{14,10},{16,20},{18,... | collective-permute-start | bytes 110600 | tf_op jit(solution)/shard_map/ppermute | solution.py:22
  151.4 10.9 %collective-permute-start = (bf16[1,56,4608]{2,1,0:T(8,128)(2,1)S(1)}, bf16[1,56,4608]{2,1,0:T(8,128)(2,1)S(1)}, u32[]{:S(2)}, u32[]{:S(2)}) collective-permute-start(bf16[1,56,4608]{2,1,0:T(8,128)(2,1)S(1)} %bitcast.107), channel_id=1, source_target_pairs={{0,2},{2,0},{4,6},{6,4},{8,10},{10,8},{12,14},{14,12},{16,18},{18,... | collective-permute-start | bytes 1548296 | tf_op jit(solution)/shard_map/ppermute | solution.py:22
  154.7 13.6 %collective-permute-start.5 = (bf16[4,1,9216]{2,0,1:T(4,128)(2,1)S(1)}, bf16[4,1,9216]{2,0,1:T(4,128)(2,1)S(1)}, u32[]{:S(2)}, u32[]{:S(2)}) collective-permute-start(bf16[4,1,9216]{2,0,1:T(4,128)(2,1)S(1)} %pad_maximum_fusion.3), channel_id=1, source_target_pairs={{0,8},{2,10},{4,12},{6,14},{8,0},{10,2},{12,4},{14,6},{16,24},{18,... | collective-permute-start | bytes 221192 | tf_op jit(solution)/shard_map/ppermute | solution.py:22
  163.4 50.6 %collective-permute-start.1 = (bf16[2,56,4608]{2,1,0:T(8,128)(2,1)}, bf16[2,56,4608]{2,1,0:T(8,128)(2,1)}, u32[]{:S(2)}, u32[]{:S(2)}) collective-permute-start(bf16[2,56,4608]{2,1,0:T(8,128)(2,1)} %pad_maximum_fusion.1), channel_id=1, source_target_pairs={{0,4},{2,6},{4,0},{6,2},{8,12},{10,14},{12,8},{14,10},{16,20},{18,... | collective-permute-start | bytes 3096584 | tf_op jit(solution)/shard_map/ppermute | solution.py:22
  168.7 48.0 %copy-start.16 = (bf16[128,576]{1,0:T(8,128)(2,1)}, bf16[128,576]{1,0:T(8,128)(2,1)S(1)}, u32[]{:S(2)}) copy-start(bf16[128,576]{1,0:T(8,128)(2,1)S(1)} %reshape.534) | copy-start | bytes 442372
  216.6 99.4 %collective-permute-start.2 = (bf16[4,56,4608]{2,1,0:T(8,128)(2,1)}, bf16[4,56,4608]{2,1,0:T(8,128)(2,1)}, u32[]{:S(2)}, u32[]{:S(2)}) collective-permute-start(bf16[4,56,4608]{2,1,0:T(8,128)(2,1)} %pad_maximum_fusion), channel_id=1, source_target_pairs={{0,8},{2,10},{4,12},{6,14},{8,0},{10,2},{12,4},{14,6},{16,24},{18,... | collective-permute-start | bytes 6193160 | tf_op jit(solution)/shard_map/ppermute | solution.py:22
  235.9 1.5 copy-start.5
  332.2 1.1 copy-start.6
  333.3 1.1 copy-start.4
  336.6 1.2 copy-start.1
  336.7 1.3 copy-start.2
  338.1 1.1 copy-start.8
  338.5 1.1 copy-start.7
  339.6 1.1 copy-start.10
  342.8 1.1 copy-start.13
  (7 other events, 7.2 us)
where the time goes:
time: 350 us; the launch traced here: 349 us
  waiting for transfers between devices  163 us (47%)
  blocking collectives  68.5 us (20%)
  local copies, waits for them, and re-layouts  53.2 us (15%)
  starting transfers between devices  39.7 us (11%)
  matrix products  12.5 us (4%)
  other arithmetic  10.5 us (3%)
    ppermute x6, waiting for transfers between devices, from_partner(): return lax.ppermute(value, axis, pairs)  122 us
    all_to_all x2, blocking collectives, moved_by_axis(): lax.all_to_all(parts, axes[k], split_axis=k, concat_axis=k, tiled=True)  68.5 us
    all_to_all x1, waiting for transfers between devices, shards(): lax.all_to_all(page_rows, DP, split_axis=0, concat_axis=0, tiled=True)  40.7 us
    ppermute x6, starting transfers between devices, from_partner(): return lax.ppermute(value, axis, pairs)  29 us
    another operation x16, local copies, waits for them, and re-layouts, shards(): gathered_pages[slot_index].reshape(-1, compressed_width)  21.2 us
    unnamed x54, local copies, waits for them, and re-layouts  20.1 us
    all_to_all x1, starting transfers between devices, shards(): lax.all_to_all(page_rows, DP, split_axis=0, concat_axis=0, tiled=True)  10.7 us
    dot_general x9, matrix products, attend(): jnp.einsum('shr,kr->shk', queries, key_matrix, preferred_element_type=jnp...  7.19 us
  transfers between devices with their start and end apart: 7, of which 4 were waited for; matrix products, arithmetic and copies ran while one was open for 9% of the time, Pallas kernels for 0%

commit v1 on v0

v1 whole, which is shorter than its diff:
```python
import functools
import math

import jax
import jax.numpy as jnp
from jax import lax
from jax.experimental import pallas as pl
from jax.experimental.pallas import tpu as pltpu
from jax.sharding import Mesh
from jax.sharding import PartitionSpec as P

LATENT_WIDTH = 512
ROTARY_WIDTH = 64
KEY = LATENT_WIDTH + ROTARY_WIDTH
PAIR = 2 * KEY
WIDE = LATENT_WIDTH + 2 * ROTARY_WIDTH
LANES = 128
TEAM_RANKS = 8
GROUPS_DP = ("groups", "dp_0", "dp_1")
MESH_ID = pl.DeviceIdType.MESH

log2_scale = 192.0 ** (-0.5) * math.log2(math.e)
masked_score = -1e30


def dot(a, b):
    return jnp.dot(a, b, preferred_element_type=jnp.float32)


def dot_t(a, b):
    return lax.dot_general(a, b, (((1,), (1,)), ((), ())), preferred_element_type=jnp.float32)


def iota(shape, dim):
    return lax.broadcasted_iota(jnp.int32, shape, dim)


def gather_kernel(
    Z,
    X,
    pool_ref,
    req_ref,
    sel_ref,
    suffix_ref,
    keys_ref,
    suf_ref,
    half_ref,
    c_ref,
    t_ref,
    w_ref,
    sendz,
    recvz,
    sendx,
    recvx,
    pool_sem,
    c_send,
    c_recv,
    w_send,
    w_recv,
    s_send,
    s_recv,
    z_send,
    z_recv,
    x_send,
    x_recv,
    r_send,
    r_recv,
    l_send,
    l_recv,
    d_send,
    d_recv,
):
    my_z = lax.axis_index("dp_0")
    my_x = lax.axis_index("dp_1")
    my_c = lax.axis_index("tp")
    half = half_ref.shape[1]
    right_hops = X // 2
    left_hops = X - 1 - right_hops
    zs = list(range(1, Z))
    xs = list(range(1, X))

    def at_z(d):
        return {"dp_0": lax.rem(my_z + d + Z, Z)}

    def at_x(e):
        return {"dp_1": lax.rem(my_x + e + X, X)}

    sibling = {"tp": 1 - my_c}

    def remote(src, dst, send, recv, where):
        return pltpu.make_async_remote_copy(
            src_ref=src, dst_ref=dst, send_sem=send, recv_sem=recv, device_id=where, device_id_type=MESH_ID
        )

    barrier = pltpu.get_barrier_semaphore()
    for d in zs:
        pl.semaphore_signal(barrier, inc=1, device_id=at_z(d), device_id_type=MESH_ID)
    for e in xs:
        pl.semaphore_signal(barrier, inc=1, device_id=at_x(e), device_id_type=MESH_ID)
    pl.semaphore_signal(barrier, inc=1, device_id=sibling, device_id_type=MESH_ID)
    start = pl.multiple_of(my_c * half, LANES)
    load = pltpu.make_async_copy(pool_ref.at[:, pl.ds(start, half)], half_ref, pool_sem)
    load.start()
    pl.semaphore_wait(barrier, len(zs) + len(xs) + 1)

    c_copies = [remote(req_ref, c_ref.at[e], c_send.at[e], c_recv.at[e], at_x(-e)) for e in xs]
    for copy in c_copies:
        copy.start()
    s_copies = [remote(suffix_ref, suf_ref.at[e], s_send.at[e], s_recv.at[e], at_x(e)) for e in xs]
    for copy in s_copies:
        copy.start()
    suf_ref[0] = suffix_ref[...]
    for copy in c_copies:
        copy.wait_recv()
    rows = [req_ref[...]] + [c_ref[e] for e in xs]
    c_all = jnp.concatenate(rows + [jnp.zeros((LANES - X, LANES), jnp.float32)], axis=0)
    lane = iota((LANES, LANES), 1)
    row = iota((LANES, LANES), 0)
    c_mine = jnp.where(lane // Z == row, c_all, 0.0).astype(jnp.bfloat16)
    pick = (iota((Z, LANES), 1) % Z == iota((Z, LANES), 0)).astype(jnp.bfloat16)
    table = dot_t(pick, c_mine)
    for d in range(Z):
        t_ref[d] = table[d : d + 1, :]

    w_copies = [remote(t_ref.at[d], w_ref.at[d], w_send.at[d], w_recv.at[d], at_z(-d)) for d in zs]
    for copy in w_copies:
        copy.start()
    w_ref[0] = t_ref[0]
    load.wait()
    for copy in w_copies:
        copy.wait_recv()
    spread = jnp.concatenate([jnp.broadcast_to(w_ref[d], (X, LANES)) for d in range(Z)], axis=0)
    lane_g = iota((Z * X, LANES), 1)
    row_g = iota((Z * X, LANES), 0)
    wanted = jnp.sum(jnp.where(lane_g == row_g % X, spread, 0.0), axis=1, keepdims=True).astype(jnp.int32)
    pages = pool_ref.shape[0]
    gather = (wanted == iota((Z * X, pages), 1) + 1).astype(jnp.bfloat16)

    z_copies = []
    for j in range(2):
        taken = dot(gather, half_ref[:, j * PAIR : (j + 1) * PAIR])
        sendz[j] = taken.reshape(Z, X, PAIR).astype(jnp.bfloat16)
        copies = [remote(sendz.at[j, d], recvz.at[j, d], z_send.at[j, d], z_recv.at[j, d], at_z(d)) for d in zs]
        for copy in copies:
            copy.start()
        recvz[j, 0] = sendz[j, 0]
        z_copies.append(copies)

    turn = (
        (iota((X * Z, Z * X), 1) % X == iota((X * Z, Z * X), 0) // Z)
        & (iota((X * Z, Z * X), 1) // X == iota((X * Z, Z * X), 0) % Z)
    ).astype(jnp.bfloat16)
    ended = []
    for j in range(2):
        for copy in z_copies[j]:
            copy.wait_recv()
        arrived = recvz[j].astype(jnp.float32).reshape(Z * X, PAIR).astype(jnp.bfloat16)
        turned = dot(turn, arrived)
        sendx[j] = turned.reshape(X, Z, PAIR).astype(jnp.bfloat16)
        x_copies = [remote(sendx.at[j, e], recvx.at[j, e], x_send.at[j, e], x_recv.at[j, e], at_x(e)) for e in xs]
        for copy in x_copies:
            copy.start()
        recvx[j, 0] = sendx[j, 0]
        for copy in x_copies:
            copy.wait_recv()
        arrived = recvx[j].astype(jnp.float32).reshape(X * Z, PAIR).astype(jnp.bfloat16)
        own = dot(sel_ref[:, : X * Z], arrived).astype(jnp.bfloat16)
        keys_ref[j, 0] = own

        def to_right(i, j=j):
            return remote(keys_ref.at[j, i - 1], keys_ref.at[j, i], r_send.at[j, i], r_recv.at[j, i], at_x(1))

        def to_left(i, j=j):
            return remote(
                keys_ref.at[j, (X - i + 1) % X], keys_ref.at[j, X - i], l_send.at[j, i], l_recv.at[j, i], at_x(-1)
            )

        def across(s, j=j):
            return remote(keys_ref.at[j, s], keys_ref.at[2 + j, s], d_send.at[j, s], d_recv.at[j, s], sibling)

        started = []

        def go(copy):
            copy.start()
            started.append(copy)

        go(to_right(1))
        go(to_left(1))
        crossing = [across(0)]
        crossing[0].start()
        for i in range(1, right_hops + 1):
            to_right(i).wait_recv()
            if i < right_hops:
                go(to_right(i + 1))
            crossing.append(across(i))
            crossing[-1].start()
            if i <= left_hops:
                to_left(i).wait_recv()
                if i < left_hops:
                    go(to_left(i + 1))
                crossing.append(across(X - i))
                crossing[-1].start()
        ended.append((x_copies, started, crossing))

    for copy in c_copies + w_copies + z_copies[0] + z_copies[1]:
        copy.wait_send()
    for copy in s_copies:
        copy.wait()
    for x_copies, started, crossing in ended:
        for copy in x_copies + started:
            copy.wait_send()
        for copy in crossing:
            copy.wait()


def gather_keys(pool, req, sel, suffix, Z, X):
    pages = pool.shape[0]
    pull = sel.shape[0]
    half = pool.shape[1] // 2
    vmem = pl.BlockSpec(memory_space=pltpu.VMEM)
    dma = pltpu.SemaphoreType.DMA
    right_hops = X // 2
    return pl.pallas_call(
        functools.partial(gather_kernel, Z, X),
        out_shape=(
            jax.ShapeDtypeStruct((4, X, pull, PAIR), jnp.bfloat16),
            jax.ShapeDtypeStruct((X, *suffix.shape), jnp.bfloat16),
        ),
        in_specs=[pl.BlockSpec(memory_space=pl.ANY), vmem, vmem, vmem],
        out_specs=(vmem, vmem),
        scratch_shapes=[
            pltpu.VMEM((pages, half), jnp.bfloat16),
            pltpu.VMEM((X, 1, LANES), jnp.float32),
            pltpu.VMEM((Z, 1, LANES), jnp.float32),
            pltpu.VMEM((Z, 1, LANES), jnp.float32),
            pltpu.VMEM((2, Z, X, PAIR), jnp.bfloat16),
            pltpu.VMEM((2, Z, X, PAIR), jnp.bfloat16),
            pltpu.VMEM((2, X, Z, PAIR), jnp.bfloat16),
            pltpu.VMEM((2, X, Z, PAIR), jnp.bfloat16),
            dma,
            dma((X,)),
            dma((X,)),
            dma((Z,)),
            dma((Z,)),
            dma((X,)),
            dma((X,)),
            dma((2, Z)),
            dma((2, Z)),
            dma((2, X)),
            dma((2, X)),
            dma((2, right_hops + 1)),
            dma((2, right_hops + 1)),
            dma((2, right_hops + 1)),
            dma((2, right_hops + 1)),
            dma((2, X)),
            dma((2, X)),
        ],
        compiler_params=pltpu.CompilerParams(collective_id=0, has_side_effects=True),
        name="gather_keys",
    )(pool, req, sel, suffix)


def both_forms(low, high):
    low_lane = iota(low.shape, 1)
    low = jnp.where(low_lane < KEY, low.astype(jnp.float32), 0.0)
    high = jnp.where(low_lane >= ROTARY_WIDTH, high.astype(jnp.float32), 0.0)
    low_moved = pltpu.roll(low, ROTARY_WIDTH, 1)
    high_moved = pltpu.roll(high, WIDE - ROTARY_WIDTH, 1)
    cast = lambda a: a.astype(jnp.bfloat16)
    return cast(low), cast(low_moved), cast(high_moved), cast(high)


def finish(acc_first, acc_second, denominator):
    moved = pltpu.roll(acc_second, WIDE - ROTARY_WIDTH, 1)
    return (acc_first + moved[:, :LATENT_WIDTH]) / denominator


def prefill_kernel(X, len_ref, q_ref, keys_ref, suf_ref, out_ref, q_first, q_second):
    tokens = q_ref.shape[0]
    heads = q_ref.shape[1] // KEY
    my_x = lax.axis_index("dp_1")
    length = len_ref[0]
    for hp in range(heads // 2):
        low = q_ref[:, hp * PAIR : hp * PAIR + WIDE]
        high = q_ref[:, hp * PAIR + LATENT_WIDTH : (hp + 1) * PAIR]
        first_low, second_low, first_high, second_high = both_forms(low, high)
        q_first[2 * hp] = first_low
        q_second[2 * hp] = second_low
        q_first[2 * hp + 1] = first_high
        q_second[2 * hp + 1] = second_high

    block = 2
    share = suf_ref.shape[0] // X

    def step(b, _):
        rows = block * tokens
        queries = [
            q_first[pl.ds(b * block, block)].reshape(rows, WIDE),
            q_second[pl.ds(b * block, block)].reshape(rows, WIDE),
        ]
        pieces = []
        for par in range(2):
            s = dot_t(queries[par], suf_ref[:, par * LATENT_WIDTH : par * LATENT_WIDTH + WIDE]) * log2_scale
            lane = iota(s.shape, 1)
            token = iota(s.shape, 0) % tokens
            rank = lax.rem(my_x - lane // share + X, X)
            pos = rank * (2 * share) + 2 * (lane % share) + par
            pieces.append(jnp.where((pos <= token) & (pos < length), s, masked_score))
        for p in range(keys_ref.shape[0]):
            for par in range(2):
                k = keys_ref[p, :, par * LATENT_WIDTH : par * LATENT_WIDTH + WIDE]
                pieces.append(dot_t(queries[par], k) * log2_scale)
        peak = functools.reduce(jnp.maximum, [jnp.max(s, axis=1, keepdims=True) for s in pieces])
        total = jnp.zeros((rows, 1), jnp.float32)
        acc = [jnp.zeros((rows, LATENT_WIDTH), jnp.float32), jnp.zeros((rows, WIDE), jnp.float32)]
        for n, s in enumerate(pieces):
            par = n % 2
            powers = jnp.exp2(s - peak)
            total = total + jnp.sum(powers, axis=1, keepdims=True)
            width = LATENT_WIDTH if par == 0 else WIDE
            source = suf_ref if n < 2 else keys_ref.at[n // 2 - 1]
            v = source[:, par * LATENT_WIDTH : par * LATENT_WIDTH + width]
            acc[par] = acc[par] + dot(powers.astype(jnp.bfloat16), v)
        result = finish(acc[0], acc[1], total)
        token = iota(result.shape, 0) % tokens
        result = jnp.where(token < length, result, 0.0).astype(jnp.bfloat16)
        for h in range(block):
            at = pl.multiple_of((b * block + h) * LATENT_WIDTH, LANES)
            out_ref[:, pl.ds(at, LATENT_WIDTH)] = result[h * tokens : (h + 1) * tokens]
        return 0

    lax.fori_loop(0, heads // block, step, 0)


def prefill(length, queries, keys, suffix, X):
    tokens = queries.shape[0]
    heads = queries.shape[1] // KEY
    vmem = pl.BlockSpec(memory_space=pltpu.VMEM)
    return pl.pallas_call(
        functools.partial(prefill_kernel, X),
        out_shape=jax.ShapeDtypeStruct((tokens, heads * LATENT_WIDTH), jnp.bfloat16),
        in_specs=[pl.BlockSpec(memory_space=pltpu.SMEM), vmem, vmem, vmem],
        out_specs=vmem,
        scratch_shapes=[
            pltpu.VMEM((heads, tokens, WIDE), jnp.bfloat16),
            pltpu.VMEM((heads, tokens, WIDE), jnp.bfloat16),
        ],
        name="prefill",
    )(length, queries, keys, suffix)


def decode_kernel(len_ref, q_ref, pool_ref, out_ref):
    decode_rows = len_ref.shape[0]
    pages = pool_ref.shape[0]
    row_pages = pages // decode_rows
    head_pairs = q_ref.shape[0] // decode_rows
    first_low, second_low, first_high, second_high = both_forms(q_ref[:, :WIDE], q_ref[:, LATENT_WIDTH:])
    queries = [
        jnp.concatenate([first_low, first_high], axis=0),
        jnp.concatenate([second_low, second_high], axis=0),
    ]
    count = 2 * q_ref.shape[0]
    page = iota((count, pages), 1)
    owner = (iota((count, pages), 0) % q_ref.shape[0]) // head_pairs
    limit = jnp.zeros((count, pages), jnp.int32)
    for r in range(decode_rows):
        limit = jnp.where(owner == r, len_ref[r], limit)
    limit = jnp.where(page // row_pages == owner, limit, 0)
    page_tokens = pool_ref.shape[1] // KEY
    pieces = []
    for n in range(page_tokens):
        at = (n // 2) * PAIR + (n % 2) * LATENT_WIDTH
        s = dot_t(queries[n % 2], pool_ref[:, at : at + WIDE]) * log2_scale
        pieces.append(jnp.where((page % row_pages) * page_tokens + n < limit, s, masked_score))
    peak = functools.reduce(jnp.maximum, [jnp.max(s, axis=1, keepdims=True) for s in pieces])
    total = jnp.zeros((count, 1), jnp.float32)
    acc = [jnp.zeros((count, LATENT_WIDTH), jnp.float32), jnp.zeros((count, WIDE), jnp.float32)]
    for n in range(page_tokens):
        at = (n // 2) * PAIR + (n % 2) * LATENT_WIDTH
        width = LATENT_WIDTH if n % 2 == 0 else WIDE
        powers = jnp.exp2(pieces[n] - peak)
        total = total + jnp.sum(powers, axis=1, keepdims=True)
        acc[n % 2] = acc[n % 2] + dot(powers.astype(jnp.bfloat16), pool_ref[:, at : at + width])
    result = finish(acc[0], acc[1], total).astype(jnp.bfloat16)
    out_ref[:, :LATENT_WIDTH] = result[: count // 2]
    out_ref[:, LATENT_WIDTH:] = result[count // 2 :]


def decode(pool, decode_queries, decode_len):
    decode_rows = decode_queries.shape[0]
    queries = decode_queries.reshape(-1, PAIR)
    vmem = pl.BlockSpec(memory_space=pltpu.VMEM)
    out = pl.pallas_call(
        decode_kernel,
        out_shape=jax.ShapeDtypeStruct((queries.shape[0], 2 * LATENT_WIDTH), jnp.bfloat16),
        in_specs=[pl.BlockSpec(memory_space=pltpu.SMEM), vmem, vmem],
        out_specs=vmem,
        name="decode",
    )(decode_len, queries, pool)
    return out.reshape(decode_rows, -1)


def shards(
    Z,
    X,
    pool,
    page_holder,
    page_slot,
    suffix_latent_rows,
    prefill_queries,
    suffix_len,
    decode_queries,
    decode_len,
):
    my_z = lax.axis_index("dp_0")
    my_x = lax.axis_index("dp_1")
    d = (my_z - page_holder // X) % Z
    e = (my_x - page_holder % X) % X
    chosen = (e * Z + d)[:, None] == jnp.arange(LANES, dtype=jnp.int32)[None, :]
    req = jnp.sum(jnp.where(chosen, page_slot[:, None] + 1, 0), axis=0)[None, :].astype(jnp.float32)
    sel = chosen.astype(jnp.bfloat16)
    suffix = suffix_latent_rows.reshape(-1, PAIR)
    keys, suf = gather_keys(pool, req, sel, suffix, Z, X)
    decode_part = decode(pool, decode_queries, decode_len)
    length = lax.dynamic_slice_in_dim(suffix_len, my_z, 1)
    keys = keys.reshape(keys.shape[0], -1, PAIR)
    suf = suf.reshape(-1, PAIR)
    prefill_part = prefill(length, prefill_queries[0], keys, suf, X)
    return (prefill_part[None], decode_part)


def solution(mesh):
    groups, dp, tp = (mesh.shape[name] for name in ("groups", "dp", "tp"))
    X = TEAM_RANKS
    Z = dp // X
    torus = Mesh(mesh.devices.reshape(groups, Z, X, tp), ("groups", "dp_0", "dp_1", "tp"))
    placed = (
        P(GROUPS_DP, None),
        P(GROUPS_DP),
        P(GROUPS_DP),
        P(GROUPS_DP, None),
        P(GROUPS_DP, None, "tp"),
        P("groups"),
        P(GROUPS_DP, "tp"),
        P(GROUPS_DP),
    )
    return jax.shard_map(
        functools.partial(shards, Z, X),
        mesh=torus,
        in_specs=placed,
        out_specs=(P(GROUPS_DP, None, "tp"), P(GROUPS_DP, "tp")),
        check_vma=False,
    )
```

time: 350 us -> 164 us (0.47)
  waiting for transfers between devices: 163 us -> 0 us
  Pallas kernels: 0 us -> 154 us
  blocking collectives: 68.5 us -> 0 us
  local copies, waits for them, and re-layouts: 53.2 us -> 4.28 us
  starting transfers between devices: 39.7 us -> 0 us
  matrix products: 12.5 us -> 0 us
  other arithmetic: 10.5 us -> 2.96 us
    pallas_call x0 -> x3, Pallas kernels: none -> 154 us  [the longest x1 139 us: gather_keys(): pl.pallas_call(functools.partial(gather_kernel, Z, X), out_shape=(jax.Sha...]
    ppermute x6 -> x0, waiting for transfers between devices: 122 us -> none  [from_partner(): return lax.ppermute(value, axis, pairs)]
    all_to_all x2 -> x0, blocking collectives: 68.5 us -> none  [moved_by_axis(): lax.all_to_all(parts, axes[k], split_axis=k, concat_axis=k, tiled=True)]
    all_to_all x1 -> x0, waiting for transfers between devices: 40.7 us -> none  [shards(): lax.all_to_all(page_rows, DP, split_axis=0, concat_axis=0, tiled=True)]
    ppermute x6 -> x0, starting transfers between devices: 29 us -> none  [from_partner(): return lax.ppermute(value, axis, pairs)]
    another operation x16 -> x0, local copies, waits for them, and re-layouts: 21.2 us -> none  [shards(): gathered_pages[slot_index].reshape(-1, compressed_width)]
    unnamed x54 -> x2, local copies, waits for them, and re-layouts: 20.1 us -> 0.01 us
    dot_general x20 -> x0, matrix products: 12.5 us -> none  [the longest x9 7.19 us: attend(): jnp.einsum('shr,kr->shk', queries, key_matrix, preferred_element_type=jnp...]
  transfers between devices with their start and end apart: 7 -> 0, of which waited for: 4 -> 0; matrix products, arithmetic and copies ran while one was open for 9% -> 0% of each run, Pallas kernels for 0% -> 0%
where the time goes in v1:
time: 164 us; the launch traced here: 162 us
  Pallas kernels  154 us (94%)
  local copies, waits for them, and re-layouts  4.28 us (3%)
  other arithmetic  2.96 us (2%)
    pallas_call x1, Pallas kernels, gather_keys(): pl.pallas_call(functools.partial(gather_kernel, Z, X), out_shape=(jax.Sha...  139 us
    pallas_call x1, Pallas kernels, prefill(): pl.pallas_call(functools.partial(prefill_kernel, X), out_shape=jax.ShapeD...  12.6 us

profile of v1, /device:TPU:65, one launch (start us, length us, event | category | flops | bytes accessed | tf_op | source)
XLA Modules:
  0.0 162.3 jit_solution(5162101791494437567)
XLA Ops:
  0.6 0.0 copy-start
  0.6 0.7 fusion.1
  1.4 0.1 select_reduce_fusion
  1.5 0.6 convert_bitcast_fusion.req_ref
  2.1 0.7 fusion.sel_ref
  2.7 0.9 reduce
  3.6 0.7 reshape.31.suffix_ref
  4.3 138.5 %gather_keys.1 = (bf16[4,8,56,1152]{3,2,1,0:T(8,128)(2,1)}, bf16[8,8,1152]{2,1,0:T(8,128)(2,1)}) custom-call(bf16[128,4608]{1,0:T(8,128)(2,1)} %pool_ref.3, f32[1,128]{1,0:T(1,128)} %convert_bitcast_fusion.req_ref, bf16[56,128]{1,0:T(8,128)(2,1)} %fusion.sel_ref, bf16[8,1152]{1,0:T(8,128)(2,1)} %reshape.31.suffix_ref), custom_call_target="tpu_custom_call" | custom-call | tf_op jit(solution)/shard_map/gather_keys/pallas_call | solution.py:223
  142.8 1.2 dynamic_slice.3.len_ref
  144.0 12.6 %prefill.1 = bf16[128,2048]{1,0:T(8,128)(2,1)} custom-call(s32[1]{0:T(128)} %dynamic_slice.3.len_ref, bf16[128,2304]{1,0:T(8,128)(2,1)} %bitcast.7, bf16[4,448,1152]{2,1,0:T(8,128)(2,1)} %bitcast.6, bf16[64,1152]{1,0:T(8,128)(2,1)} %bitcast.9), custom_call_target="tpu_custom_call" | custom-call | tf_op jit(solution)/shard_map/prefill/pallas_call | solution.py:339
  156.6 0.0 copy-done
  156.6 0.7 reshape.34.q_ref
  157.4 3.3 %decode.1 = bf16[64,1024]{1,0:T(8,128)(2,1)} custom-call(s32[4]{0:T(128)} %len_ref.1, bf16[64,1152]{1,0:T(8,128)(2,1)} %reshape.34.q_ref, bf16[128,4608]{1,0:T(8,128)(2,1)} %pool_ref.3), custom_call_target="tpu_custom_call" | custom-call | tf_op jit(solution)/shard_map/decode/pallas_call | solution.py:393
  160.6 1.6 %reshape.35 = bf16[4,16384]{1,0:T(4,128)(2,1)} reshape(bf16[64,1024]{1,0:T(8,128)(2,1)} %decode.1) | data formatting | bytes 262144 | tf_op jit(solution)/shard_map/reshape | solution.py:400
Async XLA Ops:
  0.6 156.0 %copy-start = (bf16[4,18432]{1,0:T(4,128)(2,1)S(1)}, bf16[4,18432]{1,0:T(4,128)(2,1)}, u32[]{:S(2)}) copy-start(bf16[4,18432]{1,0:T(4,128)(2,1)} %param.14) | copy-start | bytes 442372

commit v2 on v1

v2 whole, which is shorter than its diff:
```python
import functools
import math

import jax
import jax.numpy as jnp
from jax import lax
from jax.experimental import pallas as pl
from jax.experimental.pallas import tpu as pltpu
from jax.sharding import Mesh
from jax.sharding import PartitionSpec as P

LATENT_WIDTH = 512
ROTARY_WIDTH = 64
KEY = LATENT_WIDTH + ROTARY_WIDTH
PAIR = 2 * KEY
WIDE = LATENT_WIDTH + 2 * ROTARY_WIDTH
LANES = 128
TEAM_RANKS = 8
HEAD_BLOCK = 2
RIGHT_HOPS = (4, 3, 4, 3)
GROUPS_DP = ("groups", "dp_0", "dp_1")
MESH_ID = pl.DeviceIdType.MESH

log2_scale = 192.0 ** (-0.5) * math.log2(math.e)
masked_score = -1e30


def dot(a, b):
    return jnp.dot(a, b, preferred_element_type=jnp.float32)


def dot_t(a, b):
    return lax.dot_general(a, b, (((1,), (1,)), ((), ())), preferred_element_type=jnp.float32)


def iota(shape, dim):
    return lax.broadcasted_iota(jnp.int32, shape, dim)


def both_forms(low, high):
    low_lane = iota(low.shape, 1)
    low = jnp.where(low_lane < KEY, low.astype(jnp.float32), 0.0)
    high = jnp.where(low_lane >= ROTARY_WIDTH, high.astype(jnp.float32), 0.0)
    low_moved = pltpu.roll(low, ROTARY_WIDTH, 1)
    high_moved = pltpu.roll(high, WIDE - ROTARY_WIDTH, 1)
    cast = lambda a: a.astype(jnp.bfloat16)
    return cast(low), cast(low_moved), cast(high_moved), cast(high)


def finish(acc_first, acc_second, denominator):
    moved = pltpu.roll(acc_second, WIDE - ROTARY_WIDTH, 1)
    return (acc_first + moved[:, :LATENT_WIDTH]) / denominator


def kernel(
    Z,
    X,
    pool_hbm,
    q_hbm,
    dq_hbm,
    holder_ref,
    slot_ref,
    suffix_ref,
    len_ref,
    dlen_ref,
    out_ref,
    dout_ref,
    pool_ref,
    q_ref,
    dq_ref,
    c_ref,
    t_ref,
    w_ref,
    suf_ref,
    sendz,
    recvz,
    sendx,
    recvx,
    keys,
    q_first,
    q_second,
    peak_ref,
    total_ref,
    acc_first,
    acc_second,
    load_sem,
    c_send,
    c_recv,
    w_send,
    w_recv,
    s_send,
    s_recv,
    z_send,
    z_recv,
    x_send,
    x_recv,
    r_send,
    r_recv,
    l_send,
    l_recv,
    d_send,
    d_recv,
):
    my_z = lax.axis_index("dp_0")
    my_x = lax.axis_index("dp_1")
    my_c = lax.axis_index("tp")
    half = pool_ref.shape[1] // 2
    pages = pool_ref.shape[0]
    pull = keys.shape[2]
    zs = list(range(1, Z))
    xs = list(range(1, X))
    spans = []
    for at in range(0, half, PAIR):
        spans += [(at, at + LATENT_WIDTH), (at + LATENT_WIDTH, at + PAIR)]

    def at_z(d):
        return {"dp_0": lax.rem(my_z + d + Z, Z)}

    def at_x(e):
        return {"dp_1": lax.rem(my_x + e + X, X)}

    sibling = {"tp": 1 - my_c}

    def remote(src, dst, send, recv, where):
        return pltpu.make_async_remote_copy(
            src_ref=src, dst_ref=dst, send_sem=send, recv_sem=recv, device_id=where, device_id_type=MESH_ID
        )

    barrier = pltpu.get_barrier_semaphore()
    for d in zs:
        pl.semaphore_signal(barrier, inc=1, device_id=at_z(d), device_id_type=MESH_ID)
    for e in xs:
        pl.semaphore_signal(barrier, inc=1, device_id=at_x(e), device_id_type=MESH_ID)
    pl.semaphore_signal(barrier, inc=1, device_id=sibling, device_id_type=MESH_ID)
    loads = [
        pltpu.make_async_copy(src, dst, load_sem.at[n])
        for n, (src, dst) in enumerate([(pool_hbm, pool_ref), (q_hbm, q_ref), (dq_hbm, dq_ref)])
    ]
    for load in loads:
        load.start()

    holder = holder_ref[...]
    steps_z = lax.rem(my_z - holder // X + Z, Z)
    steps_x = lax.rem(my_x - holder % X + X, X)
    spots = (iota((LANES, pull), 0) == steps_x * Z + steps_z).astype(jnp.bfloat16)
    slot = jnp.broadcast_to((slot_ref[...] + 1).astype(jnp.float32), (8, pull)).astype(jnp.bfloat16)
    request = dot_t(slot, spots)
    c_ref[0] = request[:1]
    share = suf_ref.shape[1]
    flat = suffix_ref[...].astype(jnp.float32)
    suf_ref[0] = jnp.concatenate([flat[:, r * PAIR : (r + 1) * PAIR] for r in range(share)], axis=0).astype(
        jnp.bfloat16
    )
    pl.semaphore_wait(barrier, len(zs) + len(xs) + 1)

    c_copies = [remote(c_ref.at[0], c_ref.at[e], c_send.at[e], c_recv.at[e], at_x(-e)) for e in xs]
    for copy in c_copies:
        copy.start()
    s_copies = [remote(suf_ref.at[0], suf_ref.at[e], s_send.at[e], s_recv.at[e], at_x(e)) for e in xs]
    for copy in s_copies:
        copy.start()
    live = (request > 0.0).astype(jnp.bfloat16)
    before = (iota((LANES, LANES), 0) < iota((LANES, LANES), 1)).astype(jnp.bfloat16)
    place = dot(live, before)[:1].astype(jnp.int32)
    select = ((iota((pull, LANES), 0) == place) & (request[:1] > 0.0)).astype(jnp.bfloat16)
    loads[1].wait()
    prepare_queries(q_ref, q_first, q_second)
    for copy in c_copies:
        copy.wait_recv()
    rows = [c_ref[e] for e in range(X)]
    c_all = jnp.concatenate(rows + [jnp.zeros((LANES - X, LANES), jnp.float32)], axis=0)
    c_mine = jnp.where(iota((LANES, LANES), 1) // Z == iota((LANES, LANES), 0), c_all, 0.0).astype(jnp.bfloat16)
    pick = (iota((Z, LANES), 1) % Z == iota((Z, LANES), 0)).astype(jnp.bfloat16)
    table = dot_t(pick, c_mine)
    for d in range(Z):
        t_ref[d] = table[d : d + 1, :]

    w_copies = [remote(t_ref.at[d], w_ref.at[d], w_send.at[d], w_recv.at[d], at_z(-d)) for d in zs]
    for copy in w_copies:
        copy.start()
    w_ref[0] = t_ref[0]
    loads[0].wait()
    loads[2].wait()
    decode_rows(dlen_ref, dq_ref, pool_ref, dout_ref)
    for copy in w_copies:
        copy.wait_recv()
    spread = jnp.concatenate([jnp.broadcast_to(w_ref[d], (X, LANES)) for d in range(Z)], axis=0)
    mine = iota((Z * X, LANES), 1) == iota((Z * X, LANES), 0) % X
    wanted = jnp.sum(jnp.where(mine, spread, 0.0), axis=1, keepdims=True).astype(jnp.int32)
    gather = (wanted == iota((Z * X, pages), 1) + 1).astype(jnp.bfloat16)

    def along_z(k):
        lo, hi = spans[k]
        return [
            remote(sendz.at[d, :, lo:hi], recvz.at[d, :, lo:hi], z_send.at[k, d], z_recv.at[k, d], at_z(d)) for d in zs
        ]

    def along_x(k):
        lo, hi = spans[k]
        return [
            remote(sendx.at[e, :, lo:hi], recvx.at[e, :, lo:hi], x_send.at[k, e], x_recv.at[k, e], at_x(e)) for e in xs
        ]

    for k, (lo, hi) in enumerate(spans):
        start = pl.multiple_of(my_c * half + lo, LANES)
        taken = dot(gather, pool_ref[:, pl.ds(start, hi - lo)])
        sendz[:, :, lo:hi] = taken.reshape(Z, X, hi - lo).astype(jnp.bfloat16)
        for copy in along_z(k):
            copy.start()
        recvz[0, :, lo:hi] = sendz[0, :, lo:hi]

    of, to = iota((X * Z, Z * X), 1), iota((X * Z, Z * X), 0)
    turn = ((of % X == to // Z) & (of // X == to % Z)).astype(jnp.bfloat16)

    def pass_on(k):
        lo, hi = spans[k]
        for copy in along_z(k):
            copy.wait_recv()
        arrived = recvz[:, :, lo:hi].astype(jnp.float32).reshape(Z * X, hi - lo).astype(jnp.bfloat16)
        sendx[:, :, lo:hi] = dot(turn, arrived).reshape(X, Z, hi - lo).astype(jnp.bfloat16)
        for copy in along_x(k):
            copy.start()
        recvx[0, :, lo:hi] = sendx[0, :, lo:hi]

    def ring(k):
        lo, hi = spans[k]
        right_hops = RIGHT_HOPS[k % 4]
        left_hops = X - 1 - right_hops
        at = lambda side, s: keys.at[side, s, :, lo:hi]

        def to_right(i):
            return remote(at(0, i - 1), at(0, i), r_send.at[k, i], r_recv.at[k, i], at_x(1))

        def to_left(i):
            return remote(at(0, (X - i + 1) % X), at(0, X - i), l_send.at[k, i], l_recv.at[k, i], at_x(-1))

        def across(s):
            return remote(at(0, s), at(1, s), d_send.at[k, s], d_recv.at[k, s], sibling)

        def begin():
            for copy in along_x(k):
                copy.wait_recv()
            arrived = recvx[:, :, lo:hi].astype(jnp.float32).reshape(X * Z, hi - lo).astype(jnp.bfloat16)
            keys[0, 0, :, lo:hi] = dot(select[:, : X * Z], arrived).astype(jnp.bfloat16)
            if right_hops:
                to_right(1).start()
            if left_hops:
                to_left(1).start()
            across(0).start()

        def hop(i):
            if i <= right_hops:
                to_right(i).wait_recv()
                if i < right_hops:
                    to_right(i + 1).start()
                across(i).start()
            if i <= left_hops:
                to_left(i).wait_recv()
                if i < left_hops:
                    to_left(i + 1).start()
                across(X - i).start()

        def arrived():
            for s in range(X):
                across(s).wait_recv()

        def end():
            for i in range(1, right_hops + 1):
                to_right(i).wait_send()
            for i in range(1, left_hops + 1):
                to_left(i).wait_send()
            for s in range(X):
                across(s).wait_send()

        return begin, hop, arrived, end, max(right_hops, left_hops)

    rings = [ring(k) for k in range(len(spans))]
    length = len_ref[my_z]
    attend = functools.partial(
        attend_pair, X, my_x, length, keys, suf_ref, q_first, q_second, peak_ref, total_ref, acc_first, acc_second, out_ref
    )
    blocks = q_first.shape[0] // HEAD_BLOCK
    n_spans, hops = len(spans), max(r[4] for r in rings)
    waiting, done_rings = [], 0
    pass_on(0)
    for tick in range(n_spans + hops):
        if tick + 1 < n_spans:
            pass_on(tick + 1)
        for k in range(n_spans):
            i = tick - k
            if i == 0:
                rings[k][0]()
            elif 1 <= i <= rings[k][4]:
                rings[k][1](i)
                if i == rings[k][4]:
                    done_rings += 1
                    if done_rings == 2:
                        for copy in s_copies:
                            copy.wait_recv()
                    if done_rings % 2 == 0:
                        waiting += [(done_rings // 2 - 1, b) for b in range(blocks)]
        if waiting:
            p, b = waiting.pop(0)
            if b == 0:
                rings[2 * p][2]()
                rings[2 * p + 1][2]()
            attend(p, b)
    for p, b in waiting:
        if b == 0:
            rings[2 * p][2]()
            rings[2 * p + 1][2]()
        attend(p, b)

    for copy in c_copies + w_copies + s_copies:
        copy.wait_send()
    for k in range(n_spans):
        for copy in along_z(k) + along_x(k):
            copy.wait_send()
        rings[k][3]()


def prepare_queries(q_ref, q_first, q_second):
    for hp in range(q_ref.shape[1] // PAIR):
        low = q_ref[:, hp * PAIR : hp * PAIR + WIDE]
        high = q_ref[:, hp * PAIR + LATENT_WIDTH : (hp + 1) * PAIR]
        first_low, second_low, first_high, second_high = both_forms(low, high)
        q_first[2 * hp] = first_low
        q_second[2 * hp] = second_low
        q_first[2 * hp + 1] = first_high
        q_second[2 * hp + 1] = second_high


def attend_pair(
    X, my_x, length, keys, suf_ref, q_first, q_second, peak_ref, total_ref, acc_first, acc_second, out_ref, p, b
):
    tokens = q_first.shape[1]
    rows = HEAD_BLOCK * tokens
    heads = slice(b * HEAD_BLOCK, (b + 1) * HEAD_BLOCK)
    queries = [q_first[heads].reshape(rows, WIDE), q_second[heads].reshape(rows, WIDE)]
    share = suf_ref.shape[1]
    last = p == keys.shape[3] // PAIR - 1
    pieces, places = [], []
    if p == 0:
        token = iota((rows, share * X), 0) % tokens
        lane = iota((rows, share * X), 1)
        rank = lax.rem(my_x - lane // share + X, X)
        for par in range(2):
            at = par * LATENT_WIDTH
            k = suf_ref[:, :, at : at + WIDE].astype(jnp.float32).reshape(X * share, WIDE).astype(jnp.bfloat16)
            s = dot_t(queries[par], k) * log2_scale
            pos = rank * (2 * share) + 2 * (lane % share) + par
            pieces.append(jnp.where((pos <= token) & (pos < length), s, masked_score))
            places.append(k)
    for side in range(2):
        for par in range(2):
            at = p * PAIR + par * LATENT_WIDTH
            k = keys[side, :, :, at : at + WIDE].reshape(-1, WIDE)
            pieces.append(dot_t(queries[par], k) * log2_scale)
            places.append(k)
    peak = functools.reduce(jnp.maximum, [jnp.max(s, axis=1, keepdims=True) for s in pieces])
    if p:
        old = peak_ref[b][:, :1]
        peak = jnp.maximum(peak, old)
        factor = jnp.exp2(old - peak)
        total = total_ref[b][:, :1] * factor
        acc = [acc_first[b] * factor, acc_second[b] * factor]
    else:
        total = jnp.zeros((rows, 1), jnp.float32)
        acc = [jnp.zeros((rows, LATENT_WIDTH), jnp.float32), jnp.zeros((rows, WIDE), jnp.float32)]
    for n, s in enumerate(pieces):
        par = n % 2
        powers = jnp.exp2(s - peak)
        total = total + jnp.sum(powers, axis=1, keepdims=True)
        acc[par] = acc[par] + dot(powers.astype(jnp.bfloat16), places[n][:, : LATENT_WIDTH if par == 0 else WIDE])
    if not last:
        peak_ref[b] = jnp.broadcast_to(peak, (rows, LANES))
        total_ref[b] = jnp.broadcast_to(total, (rows, LANES))
        acc_first[b] = acc[0]
        acc_second[b] = acc[1]
        return
    result = finish(acc[0], acc[1], total)
    token = iota(result.shape, 0) % tokens
    result = jnp.where(token < length, result, 0.0).astype(jnp.bfloat16)
    for h in range(HEAD_BLOCK):
        at = (b * HEAD_BLOCK + h) * LATENT_WIDTH
        out_ref[:, at : at + LATENT_WIDTH] = result[h * tokens : (h + 1) * tokens]


def decode_rows(len_ref, dq_ref, pool_ref, out_ref):
    n_rows = dq_ref.shape[0]
    pages = pool_ref.shape[0]
    row_pages = pages // n_rows
    head_pairs = dq_ref.shape[1] // PAIR
    half = n_rows * head_pairs
    flat = dq_ref[...].astype(jnp.float32)
    queries = jnp.concatenate([flat[:, n * PAIR : (n + 1) * PAIR] for n in range(head_pairs)], axis=0)
    first_low, second_low, first_high, second_high = both_forms(queries[:, :WIDE], queries[:, LATENT_WIDTH:])
    queries = [
        jnp.concatenate([first_low, first_high], axis=0),
        jnp.concatenate([second_low, second_high], axis=0),
    ]
    count = 2 * half
    page = iota((count, pages), 1)
    owner = iota((count, pages), 0) % n_rows
    limit = jnp.zeros((count, pages), jnp.int32)
    for r in range(n_rows):
        limit = jnp.where(owner == r, len_ref[r], limit)
    limit = jnp.where(page // row_pages == owner, limit, 0)
    page_tokens = pool_ref.shape[1] // KEY
    pieces = []
    for n in range(page_tokens):
        at = (n // 2) * PAIR + (n % 2) * LATENT_WIDTH
        s = dot_t(queries[n % 2], pool_ref[:, at : at + WIDE]) * log2_scale
        pieces.append(jnp.where((page % row_pages) * page_tokens + n < limit, s, masked_score))
    peak = functools.reduce(jnp.maximum, [jnp.max(s, axis=1, keepdims=True) for s in pieces])
    total = jnp.zeros((count, 1), jnp.float32)
    acc = [jnp.zeros((count, LATENT_WIDTH), jnp.float32), jnp.zeros((count, WIDE), jnp.float32)]
    for n in range(page_tokens):
        at = (n // 2) * PAIR + (n % 2) * LATENT_WIDTH
        width = LATENT_WIDTH if n % 2 == 0 else WIDE
        powers = jnp.exp2(pieces[n] - peak)
        total = total + jnp.sum(powers, axis=1, keepdims=True)
        acc[n % 2] = acc[n % 2] + dot(powers.astype(jnp.bfloat16), pool_ref[:, at : at + width])
    result = finish(acc[0], acc[1], total).astype(jnp.float32)
    for n in range(head_pairs):
        at = n * 2 * LATENT_WIDTH
        low = slice(n * n_rows, (n + 1) * n_rows)
        high = slice(half + n * n_rows, half + (n + 1) * n_rows)
        out_ref[:, at : at + LATENT_WIDTH] = result[low].astype(jnp.bfloat16)
        out_ref[:, at + LATENT_WIDTH : at + 2 * LATENT_WIDTH] = result[high].astype(jnp.bfloat16)


def shards(
    Z,
    X,
    pool,
    page_holder,
    page_slot,
    suffix_latent_rows,
    prefill_queries,
    suffix_len,
    decode_queries,
    decode_len,
):
    pages = pool.shape[0]
    pull = page_holder.shape[0]
    half = pool.shape[1] // 2
    tokens = prefill_queries.shape[1]
    heads = prefill_queries.shape[2] // KEY
    decode_heads = decode_queries.shape[1] // KEY
    share = suffix_latent_rows.shape[1] // PAIR
    n_spans = 2 * half // PAIR
    blocks = heads // HEAD_BLOCK
    rows = HEAD_BLOCK * tokens
    bf16, f32 = jnp.bfloat16, jnp.float32
    hbm, vmem, smem = (pl.BlockSpec(memory_space=m) for m in (pl.ANY, pltpu.VMEM, pltpu.SMEM))
    dma = pltpu.SemaphoreType.DMA
    prefill_part, decode_part = pl.pallas_call(
        functools.partial(kernel, Z, X),
        out_shape=(
            jax.ShapeDtypeStruct((tokens, heads * LATENT_WIDTH), bf16),
            jax.ShapeDtypeStruct((decode_queries.shape[0], decode_heads * LATENT_WIDTH), bf16),
        ),
        in_specs=[hbm, hbm, hbm, vmem, vmem, vmem, smem, smem],
        out_specs=(vmem, vmem),
        scratch_shapes=[
            pltpu.VMEM(pool.shape, bf16),
            pltpu.VMEM((tokens, heads * KEY), bf16),
            pltpu.VMEM(decode_queries.shape, bf16),
            pltpu.VMEM((X, 1, LANES), f32),
            pltpu.VMEM((Z, 1, LANES), f32),
            pltpu.VMEM((Z, 1, LANES), f32),
            pltpu.VMEM((X, share, PAIR), bf16),
            pltpu.VMEM((Z, X, half), bf16),
            pltpu.VMEM((Z, X, half), bf16),
            pltpu.VMEM((X, Z, half), bf16),
            pltpu.VMEM((X, Z, half), bf16),
            pltpu.VMEM((2, X, pull, half), bf16),
            pltpu.VMEM((heads, tokens, WIDE), bf16),
            pltpu.VMEM((heads, tokens, WIDE), bf16),
            pltpu.VMEM((blocks, rows, LANES), f32),
            pltpu.VMEM((blocks, rows, LANES), f32),
            pltpu.VMEM((blocks, rows, LATENT_WIDTH), f32),
            pltpu.VMEM((blocks, rows, WIDE), f32),
            dma((3,)),
            dma((X,)),
            dma((X,)),
            dma((Z,)),
            dma((Z,)),
            dma((X,)),
            dma((X,)),
            dma((n_spans, Z)),
            dma((n_spans, Z)),
            dma((n_spans, X)),
            dma((n_spans, X)),
            dma((n_spans, X)),
            dma((n_spans, X)),
            dma((n_spans, X)),
            dma((n_spans, X)),
            dma((n_spans, X)),
            dma((n_spans, X)),
        ],
        compiler_params=pltpu.CompilerParams(
            collective_id=0, has_side_effects=True, vmem_limit_bytes=60 * 1024 * 1024
        ),
        name="whole",
    )(
        pool,
        prefill_queries[0],
        decode_queries,
        page_holder[None],
        page_slot[None],
        suffix_latent_rows,
        suffix_len,
        decode_len,
    )
    return (prefill_part[None], decode_part)


def solution(mesh):
    groups, dp, tp = (mesh.shape[name] for name in ("groups", "dp", "tp"))
    X = TEAM_RANKS
    Z = dp // X
    torus = Mesh(mesh.devices.reshape(groups, Z, X, tp), ("groups", "dp_0", "dp_1", "tp"))
    placed = (
        P(GROUPS_DP, None),
        P(GROUPS_DP),
        P(GROUPS_DP),
        P(GROUPS_DP, None),
        P(GROUPS_DP, None, "tp"),
        P("groups"),
        P(GROUPS_DP, "tp"),
        P(GROUPS_DP),
    )
    return jax.shard_map(
        functools.partial(shards, Z, X),
        mesh=torus,
        in_specs=placed,
        out_specs=(P(GROUPS_DP, None, "tp"), P(GROUPS_DP, "tp")),
        check_vma=False,
    )
```

time: 164 us -> 131 us (0.80)
  Pallas kernels: 154 us -> 126 us
  other arithmetic: 2.96 us -> 0 us
    pallas_call x3 -> x1, Pallas kernels: 154 us -> 126 us  [shards(): pl.pallas_call(functools.partial(kernel, Z, X), out_shape=(jax.ShapeDtype...]
    unnamed x2, local copies, waits for them, and re-layouts: 0.01 us -> 3.49 us
    reshape x3 -> x0, local copies, waits for them, and re-layouts: 3.04 us -> none  [the longest x1 1.63 us: decode(): return out.reshape(decode_rows, -1)]
where the time goes in v2:
time: 131 us
  Pallas kernels  126 us (96%)
  local copies, waits for them, and re-layouts  3.49 us (3%)
    pallas_call x1, Pallas kernels, shards(): pl.pallas_call(functools.partial(kernel, Z, X), out_shape=(jax.ShapeDtype...  126 us
    unnamed x2, local copies, waits for them, and re-layouts  3.49 us

profile of v2, /device:TPU:65, one launch (start us, length us, event | category | flops | bytes accessed | tf_op | source)
XLA Modules:
  0.0 130.5 jit_solution(11380707986481664251)
XLA Ops:
  0.6 126.4 %whole.1 = (bf16[128,2048]{1,0:T(8,128)(2,1)}, bf16[4,16384]{1,0:T(4,128)(2,1)}) custom-call(bf16[128,4608]{1,0:T(8,128)(2,1)} %pool_hbm.1, bf16[128,2304]{1,0:T(8,128)(2,1)} %bitcast.4, bf16[4,18432]{1,0:T(4,128)(2,1)} %dq_hbm.1, s32[1,56]{1,0:T(1,128)} %bitcast.6, s32[1,56]{1,0:T(1,128)} %bitcast.7, bf16[1,9216]{1,0:T(2,128)(2,1)} %suffix_ref.1, ...), custom_call_target="tpu_custom_call" | custom-call | tf_op jit(solution)/shard_map/whole/pallas_call | solution.py:458
  127.0 1.9 %copy.12 = bf16[1,128,2048]{2,1,0:T(8,128)(2,1)} copy(bf16[1,128,2048]{2,1,0:T(8,128)(2,1)} %bitcast.5) | data formatting | bytes 1048576
  128.9 1.6 %copy.13 = bf16[4,16384]{1,0:T(4,128)(2,1)} copy(bf16[4,16384]{1,0:T(4,128)(2,1)} %get-tuple-element.9) | data formatting | bytes 262144

commit v3 on v2

--- a/solution.py
+++ b/solution.py
@@ -18,6 +18,12 @@
 TEAM_RANKS = 8
 HEAD_BLOCK = 2
 RIGHT_HOPS = (4, 3, 4, 3)
+ROUTES = ("zx", "zx", "xz", "xz")
+STEPS = (
+    "s0", "s2", "s1", "s3", "p2", "p3", "p0", "p1", "b0", "b1", "h01", "h11",
+    "b2", "h02", "h12", "h21", "b3", "h03", "h13", "h22", "h31", "h04", "h14", "h23",
+    "h32", "w0", "w1", "a00", "h24", "h33", "a01", "h34", "w2", "w3", "a10", "a11",
+)
 GROUPS_DP = ("groups", "dp_0", "dp_1")
 MESH_ID = pl.DeviceIdType.MESH
 
@@ -201,27 +207,47 @@
             remote(sendx.at[e, :, lo:hi], recvx.at[e, :, lo:hi], x_send.at[k, e], x_recv.at[k, e], at_x(e)) for e in xs
         ]
 
-    for k, (lo, hi) in enumerate(spans):
-        start = pl.multiple_of(my_c * half + lo, LANES)
-        taken = dot(gather, pool_ref[:, pl.ds(start, hi - lo)])
-        sendz[:, :, lo:hi] = taken.reshape(Z, X, hi - lo).astype(jnp.bfloat16)
+    of, to = iota((X * Z, Z * X), 1), iota((X * Z, Z * X), 0)
+    turn = ((of % X == to // Z) & (of // X == to % Z)).astype(jnp.bfloat16)
+    back = ((of % Z == to // X) & (of // Z == to % X)).astype(jnp.bfloat16)
+    orders = {"zx": (gather, select[:, : X * Z]), "xz": (None, None)}
+    orders["xz"] = tuple(
+        m.astype(jnp.bfloat16) for m in (dot(turn, gather), dot(select[:, : X * Z], turn))
+    )
+
+    def put_z(k, rows):
+        lo, hi = spans[k]
+        sendz[:, :, lo:hi] = rows.reshape(Z, X, hi - lo).astype(jnp.bfloat16)
         for copy in along_z(k):
             copy.start()
         recvz[0, :, lo:hi] = sendz[0, :, lo:hi]
 
-    of, to = iota((X * Z, Z * X), 1), iota((X * Z, Z * X), 0)
-    turn = ((of % X == to // Z) & (of // X == to % Z)).astype(jnp.bfloat16)
-
-    def pass_on(k):
-        lo, hi = spans[k]
-        for copy in along_z(k):
-            copy.wait_recv()
-        arrived = recvz[:, :, lo:hi].astype(jnp.float32).reshape(Z * X, hi - lo).astype(jnp.bfloat16)
-        sendx[:, :, lo:hi] = dot(turn, arrived).reshape(X, Z, hi - lo).astype(jnp.bfloat16)
+    def put_x(k, rows):
+        lo, hi = spans[k]
+        sendx[:, :, lo:hi] = rows.reshape(X, Z, hi - lo).astype(jnp.bfloat16)
         for copy in along_x(k):
             copy.start()
         recvx[0, :, lo:hi] = sendx[0, :, lo:hi]
 
+    def got(k, axis):
+        lo, hi = spans[k]
+        for copy in along_z(k) if axis == "z" else along_x(k):
+            copy.wait_recv()
+        ref = recvz if axis == "z" else recvx
+        return ref[:, :, lo:hi].astype(jnp.float32).reshape(X * Z, hi - lo).astype(jnp.bfloat16)
+
+    def send(k):
+        lo, hi = spans[k]
+        start = pl.multiple_of(my_c * half + lo, LANES)
+        taken = dot(orders[ROUTES[k]][0], pool_ref[:, pl.ds(start, hi - lo)])
+        (put_z if ROUTES[k] == "zx" else put_x)(k, taken)
+
+    def pass_on(k):
+        if ROUTES[k] == "zx":
+            put_x(k, dot(turn, got(k, "z")))
+        else:
+            put_z(k, dot(back, got(k, "x")))
+
     def ring(k):
         lo, hi = spans[k]
         right_hops = RIGHT_HOPS[k % 4]
@@ -238,10 +264,7 @@
             return remote(at(0, s), at(1, s), d_send.at[k, s], d_recv.at[k, s], sibling)
 
         def begin():
-            for copy in along_x(k):
-                copy.wait_recv()
-            arrived = recvx[:, :, lo:hi].astype(jnp.float32).reshape(X * Z, hi - lo).astype(jnp.bfloat16)
-            keys[0, 0, :, lo:hi] = dot(select[:, : X * Z], arrived).astype(jnp.bfloat16)
+            keys[0, 0, :, lo:hi] = dot(orders[ROUTES[k]][1], got(k, ROUTES[k][1])).astype(jnp.bfloat16)
             if right_hops:
                 to_right(1).start()
             if left_hops:
@@ -280,36 +303,25 @@
         attend_pair, X, my_x, length, keys, suf_ref, q_first, q_second, peak_ref, total_ref, acc_first, acc_second, out_ref
     )
     blocks = q_first.shape[0] // HEAD_BLOCK
-    n_spans, hops = len(spans), max(r[4] for r in rings)
-    waiting, done_rings = [], 0
-    pass_on(0)
-    for tick in range(n_spans + hops):
-        if tick + 1 < n_spans:
-            pass_on(tick + 1)
-        for k in range(n_spans):
-            i = tick - k
-            if i == 0:
-                rings[k][0]()
-            elif 1 <= i <= rings[k][4]:
+    n_spans = len(spans)
+    for copy in s_copies:
+        copy.wait_recv()
+    for step in STEPS:
+        what, numbers = step[0], [int(n) for n in step[1:]]
+        if what == "s":
+            send(*numbers)
+        elif what == "p":
+            pass_on(*numbers)
+        elif what == "b":
+            rings[numbers[0]][0]()
+        elif what == "h":
+            k, i = numbers
+            if i <= rings[k][4]:
                 rings[k][1](i)
-                if i == rings[k][4]:
-                    done_rings += 1
-                    if done_rings == 2:
-                        for copy in s_copies:
-                            copy.wait_recv()
-                    if done_rings % 2 == 0:
-                        waiting += [(done_rings // 2 - 1, b) for b in range(blocks)]
-        if waiting:
-            p, b = waiting.pop(0)
-            if b == 0:
-                rings[2 * p][2]()
-                rings[2 * p + 1][2]()
-            attend(p, b)
-    for p, b in waiting:
-        if b == 0:
-            rings[2 * p][2]()
-            rings[2 * p + 1][2]()
-        attend(p, b)
+        elif what == "w":
+            rings[numbers[0]][2]()
+        elif what == "a":
+            attend(*numbers)
 
     for copy in c_copies + w_copies + s_copies:
         copy.wait_send()
@@ -428,6 +440,18 @@
         high = slice(half + n * n_rows, half + (n + 1) * n_rows)
         out_ref[:, at : at + LATENT_WIDTH] = result[low].astype(jnp.bfloat16)
         out_ref[:, at + LATENT_WIDTH : at + 2 * LATENT_WIDTH] = result[high].astype(jnp.bfloat16)
+
+
+def hand_over(a_in, b_in, a_out, b_out, a_held, b_held, in_sem, out_sem):
+    takes = [pltpu.make_async_copy(a_in, a_held, in_sem.at[0]), pltpu.make_async_copy(b_in, b_held, in_sem.at[1])]
+    gives = [pltpu.make_async_copy(a_held, a_out, out_sem.at[0]), pltpu.make_async_copy(b_held, b_out, out_sem.at[1])]
+    for copy in takes:
+        copy.start()
+    for take, give in zip(takes, gives):
+        take.wait()
+        give.start()
+    for copy in gives:
+        copy.wait()
 
 
 def shards(
@@ -514,6 +538,20 @@
         suffix_len,
         decode_len,
     )
+    prefill_part, decode_part = pl.pallas_call(
+        hand_over,
+        out_shape=tuple(jax.ShapeDtypeStruct(a.shape, a.dtype) for a in (prefill_part, decode_part)),
+        in_specs=[hbm, hbm],
+        out_specs=(hbm, hbm),
+        scratch_shapes=[
+            pltpu.VMEM(prefill_part.shape, bf16),
+            pltpu.VMEM(decode_part.shape, bf16),
+            dma((2,)),
+            dma((2,)),
+        ],
+        compiler_params=pltpu.CompilerParams(vmem_limit_bytes=60 * 1024 * 1024),
+        name="hand_over",
+    )(prefill_part, decode_part)
     return (prefill_part[None], decode_part)
 
 

time: 131 us -> 125 us (0.954)
  local copies, waits for them, and re-layouts: 3.49 us -> 0 us
  Pallas kernels: 126 us -> 124 us
    pallas_call x1, Pallas kernels: 126 us -> 122 us  [shards(): pl.pallas_call(functools.partial(kernel, Z, X), out_shape=(jax.ShapeDtype...]
    unnamed x2 -> x0, local copies, waits for them, and re-layouts: 3.49 us -> none
    pallas_call x0 -> x1, Pallas kernels: none -> 1.9 us  [shards(): pl.pallas_call(hand_over, out_shape=tuple((jax.ShapeDtypeStruct(a.shape,...]
where the time goes in v3:
time: 125 us; the launch traced here: 124 us
  Pallas kernels  124 us (99%)
    pallas_call x1, Pallas kernels, shards(): pl.pallas_call(functools.partial(kernel, Z, X), out_shape=(jax.ShapeDtype...  122 us

profile of v3, /device:TPU:65, one launch (start us, length us, event | category | flops | bytes accessed | tf_op | source)
XLA Modules:
  0.0 124.4 jit_solution(352094221248001538)
XLA Ops:
  0.6 121.7 %whole.1 = (bf16[128,2048]{1,0:T(8,128)(2,1)}, bf16[4,16384]{1,0:T(4,128)(2,1)}) custom-call(bf16[128,4608]{1,0:T(8,128)(2,1)} %pool_hbm.1, bf16[128,2304]{1,0:T(8,128)(2,1)} %bitcast.4, bf16[4,18432]{1,0:T(4,128)(2,1)} %dq_hbm.1, s32[1,56]{1,0:T(1,128)} %bitcast.5, s32[1,56]{1,0:T(1,128)} %bitcast.6, bf16[1,9216]{1,0:T(2,128)(2,1)} %suffix_ref.1, ...), custom_call_target="tpu_custom_call" | custom-call | tf_op jit(solution)/shard_map/whole/pallas_call | solution.py:482
  122.3 1.9 %hand_over.1 = (bf16[128,2048]{1,0:T(8,128)(2,1)}, bf16[4,16384]{1,0:T(4,128)(2,1)}) custom-call(bf16[128,2048]{1,0:T(8,128)(2,1)} %get-tuple-element.6.a_in, bf16[4,16384]{1,0:T(4,128)(2,1)} %get-tuple-element.7.b_in), custom_call_target="tpu_custom_call" | custom-call | tf_op jit(solution)/shard_map/hand_over/pallas_call | solution.py:541

commit v4 on v3

--- a/solution.py
+++ b/solution.py
@@ -18,11 +18,11 @@
 TEAM_RANKS = 8
 HEAD_BLOCK = 2
 RIGHT_HOPS = (4, 3, 4, 3)
-ROUTES = ("zx", "zx", "xz", "xz")
+ROUTES = ("zx", "xz", "xz", "xz")
 STEPS = (
-    "s0", "s2", "s1", "s3", "p2", "p3", "p0", "p1", "b0", "b1", "h01", "h11",
+    "s0", "s1", "s2", "s3", "p1", "p2", "p3", "p0", "b0", "b1", "h01", "h11",
     "b2", "h02", "h12", "h21", "b3", "h03", "h13", "h22", "h31", "h04", "h14", "h23",
-    "h32", "w0", "w1", "a00", "h24", "h33", "a01", "h34", "w2", "w3", "a10", "a11",
+    "h32", "h24", "h33", "w0", "w1", "a00", "a01", "h34", "w2", "w3", "a10", "a11",
 )
 GROUPS_DP = ("groups", "dp_0", "dp_1")
 MESH_ID = pl.DeviceIdType.MESH

time: 125 us -> 121 us (0.968)
  Pallas kernels: 124 us -> 120 us
    pallas_call x1, Pallas kernels: 122 us -> 118 us  [shards(): pl.pallas_call(functools.partial(kernel, Z, X), out_shape=(jax.ShapeDtype...]
where the time goes in v4:
time: 121 us
  Pallas kernels  120 us (99%)
    pallas_call x1, Pallas kernels, shards(): pl.pallas_call(functools.partial(kernel, Z, X), out_shape=(jax.ShapeDtype...  118 us

profile of v4, /device:TPU:65, one launch (start us, length us, event | category | flops | bytes accessed | tf_op | source)
XLA Modules:
  0.0 121.2 jit_solution(4573489471209177334)
XLA Ops:
  0.6 118.5 %whole.1 = (bf16[128,2048]{1,0:T(8,128)(2,1)}, bf16[4,16384]{1,0:T(4,128)(2,1)}) custom-call(bf16[128,4608]{1,0:T(8,128)(2,1)} %pool_hbm.1, bf16[128,2304]{1,0:T(8,128)(2,1)} %bitcast.4, bf16[4,18432]{1,0:T(4,128)(2,1)} %dq_hbm.1, s32[1,56]{1,0:T(1,128)} %bitcast.5, s32[1,56]{1,0:T(1,128)} %bitcast.6, bf16[1,9216]{1,0:T(2,128)(2,1)} %suffix_ref.1, ...), custom_call_target="tpu_custom_call" | custom-call | tf_op jit(solution)/shard_map/whole/pallas_call | solution.py:482
  119.1 1.9 %hand_over.1 = (bf16[128,2048]{1,0:T(8,128)(2,1)}, bf16[4,16384]{1,0:T(4,128)(2,1)}) custom-call(bf16[128,2048]{1,0:T(8,128)(2,1)} %get-tuple-element.6.a_in, bf16[4,16384]{1,0:T(4,128)(2,1)} %get-tuple-element.7.b_in), custom_call_target="tpu_custom_call" | custom-call | tf_op jit(solution)/shard_map/hand_over/pallas_call | solution.py:541
